TPU v7x, 256 devices: a whole 4x4x8 slice. The times are simulated.
256 devices in a mesh: expert: 64 (over x, z, core), dp: 4 (over y).
Axes of the slice: x: 4, y: 4, z: 8, core: 2. Of those that a mesh axis runs over, the one named last changes fastest.
Arguments:
- tokens: bfloat16 [65536, 2048], P(('expert', 'dp')), may hold values from -256 to 256
- routes: int32 [65536, 2], P(('expert', 'dp')), may hold values from 0 to 255, all different within a row
- priority: int32 [256, 256], P(('expert', 'dp')), may hold values from 0 to 255, each once within a row
- router: bfloat16 [2048, 256], replicated, may hold values from -3 to 3
- w_in: bfloat16 [256, 2048, 1024], P(('expert', 'dp')), may hold values from -0.125 to 0.125
- w_out: bfloat16 [256, 2048, 1024], P(('expert', 'dp')), may hold values from -0.1875 to 0.1875
Outputs:
- mixed: bfloat16 [65536, 2048], P(('expert', 'dp'))
- aux_loss: float32 [], replicated
Inputs may be any that keep to these rules, and one draw needn't show every extreme that they name: `routes`: a token's two experts differ; every expert is named by some token. `priority`: each group's 256 tokens hold every rank once.
All inputs are finite; a program needn't handle non-finite values.
Results may differ from a plain program's by a relative error of at most 0.0014.
The roundings to bfloat16 on the way count: a program that leaves them out, or rounds other values in their place, can miss the bound.
Values may be sent and summed in bfloat16 or wider, within the bound.
A program may use at most 64 MiB of HBM per device.

v0:
```python
import jax
import jax.numpy as jnp
from jax import lax
from jax.sharding import Mesh
from jax.sharding import PartitionSpec as P

EXPERT_DP = ("expert_0", "expert_1", "expert_2", "dp")
EXPERT = ("expert_0", "expert_1", "expert_2")


def cut_along(shard, dim, length):
    before, after = (shard.shape[:dim], shard.shape[dim + 1 :])
    return jnp.moveaxis(shard.reshape(*before, length, -1, *after), dim, 0)


def in_order(pieces, dim):
    pieces = jnp.moveaxis(pieces, 0, dim)
    dims = pieces.shape
    return pieces.reshape(*dims[:dim], dims[dim] * dims[dim + 1], *dims[dim + 2 :])


def joined_exchange(shard, axis, axes, splits, concats):
    sizes = [lax.axis_size(a) for a in axes]
    pieces = cut_along(shard, splits[0], sizes[0])
    pieces = jnp.moveaxis(cut_along(pieces, splits[1] + 1, sizes[1]), 0, 1)
    inside = pieces.shape[2:]
    pieces = pieces.reshape(-1, *inside)
    pieces = lax.all_to_all(pieces, axis, split_axis=0, concat_axis=0, tiled=True)
    pieces = in_order(pieces.reshape(*sizes, *inside), concats[0] + 1)
    return in_order(pieces, concats[1])


def by_axis(shard, axes):
    for axis in axes:
        shard = lax.psum(shard, axis)
    return shard


def send_rows(outgoing):
    arrived = joined_exchange(outgoing, EXPERT_DP, (EXPERT, "dp"), (0, 1), (0, 1))
    return arrived


def return_rows(produced):
    returned = joined_exchange(produced, EXPERT_DP, (EXPERT, "dp"), (0, 1), (0, 1))
    return returned


def shards(tokens, routes, priority, router, w_in, w_out):
    group_rows = tokens.shape[0]
    width = tokens.shape[1]
    experts = router.shape[1]
    slot_cap = 4 * group_rows // experts
    owner_count = lax.axis_size(EXPERT)
    column_count = lax.axis_size("dp")
    logits = jnp.dot(tokens, router, preferred_element_type=jnp.float32)
    probs = jax.nn.softmax(logits, axis=-1)
    expert_grid = lax.broadcasted_iota(jnp.int32, (group_rows, experts), 1)
    first = routes[:, 0]
    second = routes[:, 1]
    first_hot = (expert_grid == first[:, None]).astype(jnp.float32)
    second_hot = (expert_grid == second[:, None]).astype(jnp.float32)
    logit_first = jnp.sum(logits * first_hot, axis=1)
    logit_second = jnp.sum(logits * second_hot, axis=1)
    gate_first = jax.nn.sigmoid(logit_first - logit_second).astype(jnp.bfloat16)
    gate_second = jax.nn.sigmoid(logit_second - logit_first).astype(jnp.bfloat16)
    ranks = priority[0]
    earlier = (ranks[None, :] < ranks[:, None]).astype(jnp.bfloat16)
    before_first = jnp.dot(
        earlier, first_hot.astype(jnp.bfloat16), preferred_element_type=jnp.float32
    )
    before_second = jnp.dot(
        earlier, second_hot.astype(jnp.bfloat16), preferred_element_type=jnp.float32
    )
    first_load = jnp.sum(first_hot, axis=0)
    pos_first = jnp.sum(before_first * first_hot, axis=1).astype(jnp.int32)
    pos_second = jnp.sum((before_second + first_load[None, :]) * second_hot, axis=1).astype(
        jnp.int32
    )
    slot_first = jnp.where(pos_first < slot_cap, first * slot_cap + pos_first, -1)
    slot_second = jnp.where(pos_second < slot_cap, second * slot_cap + pos_second, -1)
    slot_grid = lax.broadcasted_iota(jnp.int32, (experts * slot_cap, group_rows), 0)
    dispatch = ((slot_grid == slot_first[None, :]) | (slot_grid == slot_second[None, :])).astype(
        jnp.bfloat16
    )
    outgoing = jnp.dot(dispatch, tokens, preferred_element_type=jnp.float32).astype(jnp.bfloat16)
    outgoing = outgoing.reshape(owner_count, column_count, slot_cap, width)
    arrived = send_rows(outgoing)
    expert_rows = arrived.reshape(experts * slot_cap, width)
    hidden = jax.nn.relu(jnp.dot(expert_rows, w_in[0], preferred_element_type=jnp.float32)).astype(
        jnp.bfloat16
    )
    produced = lax.dot_general(
        hidden, w_out[0], (((1,), (1,)), ((), ())), preferred_element_type=jnp.float32
    ).astype(jnp.bfloat16)
    returned = return_rows(produced.reshape(owner_count, column_count, slot_cap, width))
    returned = returned.reshape(experts * slot_cap, width)
    token_grid = lax.broadcasted_iota(jnp.int32, (group_rows, experts * slot_cap), 1)
    nothing = jnp.zeros((), jnp.bfloat16)
    combine = jnp.where(
        token_grid == slot_first[:, None], gate_first[:, None], nothing
    ) + jnp.where(token_grid == slot_second[:, None], gate_second[:, None], nothing)
    mixed = jnp.dot(combine, returned, preferred_element_type=jnp.float32).astype(jnp.bfloat16)
    prob_sum = jnp.sum(probs, axis=0)
    statistics = jnp.stack([prob_sum, first_load], axis=0)
    all_tokens = group_rows * owner_count * column_count
    totals = by_axis(statistics, EXPERT_DP)
    aux_loss = experts * jnp.sum(totals[0] / all_tokens * (totals[1] / all_tokens))
    return (mixed, aux_loss)


def solution(mesh):
    torus = Mesh(
        mesh.devices.reshape(4, 8, 2, mesh.shape["dp"]), ("expert_0", "expert_1", "expert_2", "dp")
    )
    placed = (
        P(EXPERT_DP, None),
        P(EXPERT_DP, None),
        P(EXPERT_DP, None),
        P(),
        P(EXPERT_DP, None, None),
        P(EXPERT_DP, None, None),
    )
    return jax.shard_map(
        shards, mesh=torus, in_specs=placed, out_specs=(P(EXPERT_DP, None), P()), check_vma=False
    )
```

profile of v0, /device:TPU:1, one launch (start us, length us, event | category | flops | bytes accessed | tf_op | source)
XLA Modules:
  0.0 294.3 jit_solution(6869267080288702023)
XLA Ops:
  0.6 0.0 copy-start
  0.6 0.8 fusion.40
  1.4 1.1 fusion.10
  2.5 0.0 copy-done
  2.5 1.8 fusion.41
  4.3 0.1 fusion.28
  4.4 0.2 divide_reduce_fusion
  4.6 1.1 fusion.11
  5.7 3.2 %convolution_convert_fusion = bf16[1024,2048]{1,0:T(8,128)(2,1)} fusion(bf16[256,2048]{1,0:T(8,128)(2,1)S(1)} %copy-done, s32[256]{0:T(256)S(1)} %get-tuple-element.14, s32[256]{0:T(256)S(1)} %get-tuple-element.15), kind=kOutput, calls=%fused_computation.5 | convolution fusion | flops 1076625408 | bytes 5244928 | tf_op jit(solution)/shard_map/dot_general | solution.py:86
  8.9 7.2 %reshape_transpose_transpose_reshape_reshape_reshape.6 = bf16[256,1,1,4,2048]{4,3,0,2,1:T(4,128)(2,1)} reshape(bf16[1024,2048]{1,0:T(8,128)(2,1)} %convolution_convert_fusion) | data formatting | bytes 8388608 | tf_op jit(solution)/shard_map/reshape;transpose;transpose;reshape;reshape;reshape | solution.py:27
  16.1 115.2 %all_to_all.10 = bf16[256,1,1,4,2048]{4,3,2,1,0:T(4,128)(2,1)} all-to-all(bf16[256,1,1,4,2048]{4,3,2,1,0:T(4,128)(2,1)} %bitcast.46), channel_id=1, replica_groups=mesh['expert_0'=4,'expert_1'=8,'expert_2'=2,'dp'=4] {'expert_0','expert_..., dimensions={0} | all-to-all | bytes 8388608 | tf_op jit(solution)/shard_map/all_to_all | solution.py:28
  131.3 6.9 %reshape_reshape.6 = bf16[1024,2048]{1,0:T(8,128)(2,1)} reshape(bf16[64,4,1,4,2048]{4,3,1,0,2:T(4,128)(2,1)} %bitcast.47) | data formatting | bytes 8388608 | tf_op jit(solution)/shard_map/reshape;reshape | solution.py:89
  138.3 0.0 copy-start.2
  138.3 8.1 %maximum_convert_fusion = bf16[1024,1024]{1,0:T(8,128)(2,1)S(1)} fusion(bf16[1024,2048]{1,0:T(8,128)(2,1)} %reshape_reshape.6, bf16[1,2048,1024]{2,1,0:T(8,128)(2,1)} %param.10), kind=kOutput, calls=%fused_computation.4 | convolution fusion | flops 4297064448 | bytes 10485760 | tf_op jit(solution)/shard_map/dot_general | solution.py:90
  146.3 0.0 copy-done.2
  146.4 6.1 %fusion.4 = bf16[1024,2048]{1,0:T(8,128)(2,1)} fusion(bf16[1024,1024]{1,0:T(8,128)(2,1)S(1)} %maximum_convert_fusion, bf16[1,2048,1024]{2,1,0:T(8,128)(2,1)S(1)} %copy-done.2), kind=kOutput, calls=%fused_computation.6 | convolution fusion | flops 4297064448 | bytes 10485760 | tf_op jit(solution)/shard_map/dot_general | solution.py:93
  152.5 7.2 %reshape_transpose_transpose_reshape_reshape_reshape.7 = bf16[256,1,1,4,2048]{4,3,0,2,1:T(4,128)(2,1)} reshape(bf16[1024,2048]{1,0:T(8,128)(2,1)} %fusion.4) | data formatting | bytes 8388608 | tf_op jit(solution)/shard_map/reshape;transpose;transpose;reshape;reshape;reshape | solution.py:27
  159.7 0.0 copy-start.1
  159.7 8.0 %all-to-all-start.1 = ((bf16[256,1,1,4,2048]{4,3,2,1,0:T(4,128)(2,1)}), bf16[256,1,1,4,2048]{4,3,2,1,0:T(4,128)(2,1)}, u32[]{:S(2)}, u32[]{:S(2)}) async-start(bf16[256,1,1,4,2048]{4,3,2,1,0:T(4,128)(2,1)} %bitcast.45), calls=%async_computation.1 | async-start | bytes 8388608 | tf_op jit(solution)/shard_map/all_to_all | solution.py:28
  167.7 10.3 %psum.28 = f32[2,256]{1,0:T(2,128)S(1)} all-reduce(f32[2,256]{1,0:T(2,128)S(1)} %pad_maximum_fusion), channel_id=1, replica_groups=mesh['expert_0'=4,'expert_1'=8,'expert_2'=2,'dp'=4] {'expert_0'}, use_global_device_ids=true, to_apply=%region_8.9 | all-reduce | flops 512 | bytes 4096 | tf_op jit(solution)/shard_map/psum | solution.py:35
  178.0 89.1 %psum.29 = f32[2,256]{1,0:T(2,128)S(1)} all-reduce(f32[2,256]{1,0:T(2,128)S(1)} %psum.28), channel_id=1, replica_groups=mesh['expert_0'=4,'expert_1'=8,'expert_2'=2,'dp'=4] {'expert_1'}, use_global_device_ids=true, to_apply=%region_9.10 | all-reduce | flops 512 | bytes 4096 | tf_op jit(solution)/shard_map/psum | solution.py:35
  267.1 4.7 %psum.30 = f32[2,256]{1,0:T(2,128)S(1)} all-reduce(f32[2,256]{1,0:T(2,128)S(1)} %psum.29), channel_id=1, replica_groups=mesh['expert_0'=4,'expert_1'=8,'expert_2'=2,'dp'=4] {'expert_2'}, use_global_device_ids=true, to_apply=%region_10.11 | all-reduce | flops 512 | bytes 4096 | tf_op jit(solution)/shard_map/psum | solution.py:35
  271.9 8.5 %psum.31 = f32[2,256]{1,0:T(2,128)S(1)} all-reduce(f32[2,256]{1,0:T(2,128)S(1)} %psum.30), channel_id=1, replica_groups=mesh['expert_0'=4,'expert_1'=8,'expert_2'=2,'dp'=4] {'dp'}, use_global_device_ids=true, to_apply=%region_11.12 | all-reduce | flops 512 | bytes 4096 | tf_op jit(solution)/shard_map/psum | solution.py:35
  280.4 0.6 fusion.38
  281.6 0.0 copy-done.1
  281.7 0.0 all-to-all-done.1
  281.7 6.9 %reshape_reshape.7 = bf16[1024,2048]{1,0:T(8,128)(2,1)} reshape(bf16[64,4,1,4,2048]{4,3,1,0,2:T(4,128)(2,1)} %bitcast.18) | data formatting | bytes 8388608 | tf_op jit(solution)/shard_map/reshape;reshape | solution.py:97
  288.6 4.6 %convolution_convert_fusion.1 = bf16[256,2048]{1,0:T(8,128)(2,1)} fusion(bf16[1024,2048]{1,0:T(8,128)(2,1)} %reshape_reshape.7, s32[256]{0:T(256)S(1)} %bitcast.59, s32[256]{0:T(256)S(1)} %bitcast.58, bf16[256]{0:T(256)(128)(2,1)S(1)} %get-tuple-element.7, bf16[256]{0:T(256)(128)(2,1)S(1)} %get-tuple-element.6), kind=kOutput, calls=%fused_computation.7 | convolution fusion | flops 1076363264 | bytes 5245952 | tf_op jit(solution)/shard_map/dot_general | solution.py:103
  (6 shorter events, 0.0 us)
Async XLA Ops:
  0.6 1.9 copy-start
  138.3 8.1 %copy-start.2 = (bf16[1,2048,1024]{2,1,0:T(8,128)(2,1)S(1)}, bf16[1,2048,1024]{2,1,0:T(8,128)(2,1)}, u32[]{:S(2)}) copy-start(bf16[1,2048,1024]{2,1,0:T(8,128)(2,1)} %param.11) | copy-start | bytes 12582916
  159.7 121.9 %copy-start.1 = (s32[256,2]{0,1:T(2,128)S(1)}, s32[256,2]{0,1:T(2,128)}, u32[]{:S(2)}) copy-start(s32[256,2]{0,1:T(2,128)} %param.7) | copy-start | bytes 6148
  159.7 122.0 %all-to-all-start.1 = ((bf16[256,1,1,4,2048]{4,3,2,1,0:T(4,128)(2,1)}), bf16[256,1,1,4,2048]{4,3,2,1,0:T(4,128)(2,1)}, u32[]{:S(2)}, u32[]{:S(2)}) async-start(bf16[256,1,1,4,2048]{4,3,2,1,0:T(4,128)(2,1)} %bitcast.45), calls=%async_computation.1 | async-start | bytes 8388608 | tf_op jit(solution)/shard_map/all_to_all | solution.py:28
where the time goes:
time: 296 us; the launch traced here: 294 us
  blocking collectives  228 us (77%)
  local copies, waits for them, and re-layouts  29 us (10%)
  matrix products  26 us (9%)
  starting transfers between devices  7.97 us (3%)
    all_to_all x1, blocking collectives, joined_exchange(): lax.all_to_all(pieces, axis, split_axis=0, concat_axis=0, tiled=True)  115 us
    psum x4, blocking collectives, by_axis(): shard = lax.psum(shard, axis)  113 us
    another operation x2, local copies, waits for them, and re-layouts, joined_exchange(): pieces = pieces.reshape(-1, *inside)  14.4 us
    dot_general x1, matrix products, shards(): jnp.dot(expert_rows, w_in[0], preferred_element_type=jnp.float32)  8.08 us
    all_to_all x1, starting transfers between devices, joined_exchange(): lax.all_to_all(pieces, axis, split_axis=0, concat_axis=0, tiled=True)  7.97 us
    another operation x1, local copies, waits for them, and re-layouts, shards(): expert_rows = arrived.reshape(experts * slot_cap, width)  6.91 us
    another operation x1, local copies, waits for them, and re-layouts, shards(): returned = returned.reshape(experts * slot_cap, width)  6.9 us
    dot_general x1, matrix products, shards(): lax.dot_general(hidden, w_out[0], (((1,), (1,)), ((), ())), preferred_ele...  6.14 us
  transfers between devices with their start and end apart: 1, of which 0 were waited for; matrix products, arithmetic and copies ran while one was open for 0% of the time, Pallas kernels for 0%

commit v1 on v0

v1 whole, which is shorter than its diff:
```python
import jax
import jax.numpy as jnp
from jax import lax
from jax.experimental import pallas as pl
from jax.experimental.pallas import tpu as pltpu
from jax.sharding import Mesh
from jax.sharding import PartitionSpec as P

MESH = pl.DeviceIdType.MESH
EXPERT_DP = ("expert_0", "expert_1", "expert_2", "dp")
BF = jnp.bfloat16
F32 = jnp.float32
D = 2048
FF = 1024
NC = 4
L = D // NC
NONE = -1.0e6

S0 = 0
S1 = 768
S2 = S1 + 2 * 512
RX = S2 + 2 * 640
RB_ROWS = RX + 3 * 128


def iota(shape, dim):
    return lax.broadcasted_iota(jnp.int32, shape, dim)


def rows(start, count):
    return pl.ds(start if isinstance(start, int) else pl.multiple_of(start, 8), count)


def cols(c, width=L):
    return pl.ds(pl.multiple_of(c * width, width), width)


def to_col(row):
    eye = iota((256, 256), 0) == iota((256, 256), 1)
    return jnp.sum(jnp.where(eye, row, 0.0), axis=1, keepdims=True)


def to_row(col):
    eye = iota((256, 256), 0) == iota((256, 256), 1)
    return jnp.sum(jnp.where(eye, col, 0.0), axis=0, keepdims=True)


def kernel(
    t_hbm, routes, ranks, router_hbm, w1_hbm, w2_hbm, out, aux,
    T2, SRC, PK, X, Y, RB, V2, V1, W1, W2, RT, H, PM, PMK, C2, C1, C0, M, STA, STB, STC,
    ld, zs, zr, tws, twr, pks, pkr, ms, mr, xs, xr, ys, yr, sts, str_,
    gs, gr, es, er, t1s, t1r, v2s, v2r, v1s, v1r,
):
    x = lax.axis_index("expert_0")
    z = lax.axis_index("expert_1")
    k = lax.axis_index("expert_2")
    y = lax.axis_index("dp")
    me = x * 4 + y
    kt = 1 - k
    zn = [lax.rem(z + 1, 8), lax.rem(z + 7, 8)]
    zn2 = [lax.rem(z + 2, 8), lax.rem(z + 6, 8)]

    def remote(src, dst, ss, rs, **where):
        return pltpu.make_async_remote_copy(
            src_ref=src, dst_ref=dst, send_sem=ss, recv_sem=rs, device_id=where, device_id_type=MESH
        )

    def xy(i):
        d = lax.rem(me + i, 16)
        return d, {"expert_0": d // 4, "dp": lax.rem(d, 4)}

    loads = [
        pltpu.make_async_copy(t_hbm, T2.at[rows(k * 256, 256)], ld.at[0]),
        pltpu.make_async_copy(router_hbm, RT, ld.at[1]),
        pltpu.make_async_copy(w1_hbm, W1, ld.at[2]),
        pltpu.make_async_copy(w2_hbm, W2, ld.at[3]),
    ]
    for load in loads:
        load.start()

    barrier = pltpu.get_barrier_semaphore()

    @pl.loop(1, 16)
    def _(i):
        pl.semaphore_signal(barrier, inc=1, device_id=xy(i)[1], device_id_type=MESH)

    @pl.loop(1, 8)
    def _(i):
        pl.semaphore_signal(
            barrier, inc=1, device_id={"expert_1": lax.rem(z + i, 8)}, device_id_type=MESH
        )

    for other in (zn[0], zn[1], zn2[0], zn2[1], z):
        pl.semaphore_signal(
            barrier, inc=1, device_id={"expert_1": other, "expert_2": kt}, device_id_type=MESH
        )
    pl.semaphore_wait(barrier, 27)

    def t2(idx, kk):
        return rows((idx * 2 + kk) * 256, 256)

    def tok_z(u, step, c):
        src = t2(0 if step == 0 else 1 + u, k)
        dst = t2(1 + u + 2 * step, k)
        return remote(
            T2.at[src, cols(c)], T2.at[dst, cols(c)], zs.at[u, step, c], zr.at[u, step, c],
            expert_1=zn[u],
        )

    def tok_twin(idx, c):
        r = t2(idx, k)
        return remote(
            T2.at[r, cols(c)], T2.at[r, cols(c)], tws.at[idx, c], twr.at[idx, c], expert_2=kt
        )

    def slots_z(u, far, c):
        if far:
            return remote(
                PK.at[rows(u * 192 + 128, 64), cols(c)], SRC.at[rows(7 * 128 + u * 64, 64), cols(c)],
                pks.at[u, 1, c], pkr.at[u, 1, c], expert_1=zn2[u],
            )
        return remote(
            PK.at[rows(u * 192, 128), cols(c)], SRC.at[rows((5 + u) * 128, 128), cols(c)],
            pks.at[u, 0, c], pkr.at[u, 0, c], expert_1=zn[u],
        )

    def meta_to(n):
        src = M.at[rows(k * 8, 8)]
        if n == 0:
            idx, where = 0, {"expert_2": kt}
        else:
            idx, other = (n - 1) // 2 + 1, (n - 1) % 2
            target = (zn if idx < 3 else zn2)[(idx - 1) % 2]
            where = {"expert_1": target, "expert_2": kt if other else k}
        return remote(src, M.at[rows((idx * 2 + k) * 8, 8)], ms.at[n], mr.at[idx * 2 + k], **where)

    def meta_wait(idx):
        for kk in ((kt,) if idx == 0 else (0, 1)):
            r = rows((idx * 2 + kk) * 8, 8)
            remote(M.at[r], M.at[r], ms.at[0], mr.at[idx * 2 + kk], expert_2=kt).wait_recv()

    def tile_out(idx, i):
        d, where = xy(i)
        return remote(
            SRC.at[rows(idx * 128 + d * 8, 8)], X.at[rows(idx * 128 + me * 8, 8)],
            xs.at[idx], xr.at[idx], **where,
        )

    def tiles(idx):
        r = rows(idx * 128, 120)
        return remote(SRC.at[r], X.at[r], xs.at[idx], xr.at[idx], expert_2=kt)

    def scatter(idx):
        @pl.loop(1, 16)
        def _(i):
            tile_out(idx, i).start()

        own = rows(idx * 128 + me * 8, 8)
        X[own, :] = SRC[own, :]

    def home_row(idx):
        if idx == 0:
            return S0 + k * 128
        if idx < 3:
            return S1 + (idx - 1) * 512 + k * 128
        if idx < 5:
            return S2 + (idx - 3) * 640 + k * 320
        return RX + (idx - 5) * 128

    def tile_back(idx, i):
        d, where = xy(i)
        return remote(
            Y.at[rows(idx * 128 + d * 8, 8)], RB.at[rows(home_row(idx) + me * 8, 8)],
            ys.at[idx], yr.at[idx], **where,
        )

    def tiles_back(idx):
        return remote(
            Y.at[rows(idx * 128, 120)], RB.at[rows(home_row(idx), 120)], ys.at[idx], yr.at[idx],
            expert_2=kt,
        )

    def scatter_back(idx):
        @pl.loop(1, 16)
        def _(i):
            tile_back(idx, i).start()

        RB[rows(home_row(idx) + me * 8, 8), :] = Y[rows(idx * 128 + me * 8, 8), :]

    def back_z(d, far, c):
        if far:
            return remote(
                RB.at[rows(RX + 256 + d * 64, 64), cols(c)],
                RB.at[rows(S2 + d * 640 + k * 320 + 256, 64), cols(c)],
                gs.at[d, 1, c], gr.at[d, 1, c], expert_1=zn2[1 - d],
            )
        return remote(
            RB.at[rows(RX + d * 128, 128), cols(c)],
            RB.at[rows(S2 + d * 640 + k * 320 + 128, 128), cols(c)],
            gs.at[d, 0, c], gr.at[d, 0, c], expert_1=zn[1 - d],
        )

    def back_twin2(d, c):
        r = rows(S2 + d * 640 + k * 320, 320)
        return remote(RB.at[r, cols(c)], RB.at[r, cols(c)], es.at[d, c], er.at[d, c], expert_2=kt)

    def back_twin1(n):
        r = rows(home_row(n), 128)
        return remote(RB.at[r], RB.at[r], t1s.at[n], t1r.at[n], expert_2=kt)

    def mixed2(d, c):
        return remote(
            V2.at[rows(d * 256, 256), cols(c)], RB.at[rows(S1 + d * 512 + 256, 256), cols(c)],
            v2s.at[d, c], v2r.at[d, c], expert_1=zn[1 - d],
        )

    def mixed1(d, c):
        return remote(
            V1.at[rows(d * 256, 256), cols(c)], RB.at[rows(S0 + 256 + d * 256, 256), cols(c)],
            v1s.at[d, c], v1r.at[d, c], expert_1=zn[1 - d],
        )

    def stat_xy(i):
        _, where = xy(i)
        r = rows(me * 8, 8)
        return remote(STA.at[r], STA.at[r], sts.at[0], str_.at[0], **where)

    def stat_z(i):
        r = rows(z * 8, 8)
        return remote(
            STB.at[r], STB.at[r], sts.at[1], str_.at[1], expert_1=lax.rem(z + i, 8)
        )

    def stat_twin():
        r = rows(k * 8, 8)
        return remote(STC.at[r], STC.at[r], sts.at[2], str_.at[2], expert_2=kt)

    def one_hot(dst, row0, count, idx, base):
        code = (iota((count, 256), 0) + base).astype(F32)
        for g in range(2):
            r = (idx * 2 + g) * 8
            hit = (code == M[r : r + 1, :]) | (code == M[r + 1 : r + 2, :])
            dst[row0 : row0 + count, g * 256 : (g + 1) * 256] = jnp.where(hit, 1.0, 0.0).astype(BF)

    def pack(idx):
        one_hot(PM, 0, 128, idx, (z * 2 + k) * 128)

        @pl.loop(0, NC)
        def _(c):
            SRC[idx * 128 : idx * 128 + 128, cols(c)] = jnp.dot(
                PM[...], T2[idx * 512 : idx * 512 + 512, cols(c)], preferred_element_type=F32
            ).astype(BF)

    def ffn(idx, count):
        r = pl.ds(idx * 128, count * 128)
        h = pl.ds(0, count * 128)

        @pl.loop(0, FF // 256)
        def _(n):
            part = jnp.dot(X[r, :], W1[:, cols(n, 256)], preferred_element_type=F32)
            H[h, cols(n, 256)] = jnp.maximum(part, 0.0).astype(BF)

        @pl.loop(0, D // 256)
        def _(n):
            Y[r, cols(n, 256)] = lax.dot_general(
                H[h, :], W2[pl.ds(pl.multiple_of(n * 256, 256), 256), :],
                (((1,), (1,)), ((), ())), preferred_element_type=F32,
            ).astype(BF)

    def meta_cols(idx):
        block = M[rows((idx * 2 + k) * 8, 8), :]
        return [to_col(block[i : i + 1, :]) for i in range(6)]

    def weights(e1, e2, low, g1, g2):
        in1 = (e1 >= low) & (e1 <= 4.0)
        in2 = (e2 >= low) & (e2 <= 4.0)
        both = in1 & in2
        return jnp.where(both, g1, 1.0), jnp.where(both, g2, 1.0)

    def passed(e1, e2, low, w1, w2):
        in1 = (e1 >= low) & (e1 <= 4.0)
        in2 = (e2 >= low) & (e2 <= 4.0)
        return jnp.where(
            in1 & in2, 1.0, jnp.where(in1, w1, 0.0) + jnp.where(in2, w2, 0.0)
        )

    def placed(code, s1, s2, w1, w2):
        return (jnp.where(code == s1, w1, 0.0) + jnp.where(code == s2, w2, 0.0)).astype(BF)

    def diagonal(col):
        eye = iota((256, 256), 0) == iota((256, 256), 1)
        return jnp.where(eye, col, 0.0).astype(BF)

    loads[0].wait()

    @pl.loop(0, NC)
    def _(c):
        tok_z(0, 0, c).start()
        tok_z(1, 0, c).start()
        tok_twin(0, c).start()

    loads[1].wait()
    logits = jnp.dot(T2[t2(0, k), :], RT[...], preferred_element_type=F32)
    lane = iota((256, 256), 1).astype(F32)
    first_row, second_row = routes[0:1, :], routes[1:2, :]
    first_hot = jnp.where(lane == to_col(first_row.astype(F32)), 1.0, 0.0)
    second_hot = jnp.where(lane == to_col(second_row.astype(F32)), 1.0, 0.0)
    logit_first = jnp.sum(logits * first_hot, axis=1, keepdims=True)
    logit_second = jnp.sum(logits * second_hot, axis=1, keepdims=True)
    gate_first = 1.0 / (1.0 + jnp.exp(logit_second - logit_first))
    gate_second = 1.0 / (1.0 + jnp.exp(logit_first - logit_second))
    rank_row = ranks[...].astype(F32)
    earlier = jnp.where(rank_row < to_col(rank_row), 1.0, 0.0).astype(BF)
    before_first = jnp.dot(earlier, first_hot.astype(BF), preferred_element_type=F32)
    before_second = jnp.dot(earlier, second_hot.astype(BF), preferred_element_type=F32)
    first_load = jnp.sum(first_hot, axis=0, keepdims=True)
    pos_first = to_row(jnp.sum(before_first * first_hot, axis=1, keepdims=True))
    pos_second = to_row(
        jnp.sum((before_second + first_load) * second_hot, axis=1, keepdims=True)
    )

    def slot_and_side(expert, pos):
        ex, ez, ek, ey = expert >> 6, (expert >> 3) & 7, (expert >> 2) & 1, expert & 3
        base = (ez * 2 + ek) * 128 + (ex * 4 + ey) * 8 + k * 4
        away = (ez - z) & 7
        side = jnp.where(
            away < 4, away, jnp.where((away == 4) & (ex < 2), 4, away - 8)
        )
        kept = pos < 4.0
        return (
            jnp.where(kept, base.astype(F32) + pos, NONE),
            jnp.where(kept, side.astype(F32), 99.0),
        )

    slot1, side1 = slot_and_side(first_row, pos_first)
    slot2, side2 = slot_and_side(second_row, pos_second)
    zero = jnp.zeros((1, 256), F32)
    own_meta = rows(k * 8, 8)
    M[own_meta, :] = jnp.concatenate(
        [
            slot1, slot2, to_row(gate_first).astype(BF).astype(F32),
            to_row(gate_second).astype(BF).astype(F32), side1, side2, zero, zero,
        ],
        axis=0,
    )
    for n in range(9):
        meta_to(n).start()
    top = jnp.max(logits, axis=1, keepdims=True)
    raised = jnp.exp(logits - top)
    probs = raised / jnp.sum(raised, axis=1, keepdims=True)
    prob_sum = jnp.sum(probs, axis=0, keepdims=True)
    STA[rows(me * 8, 8), :] = jnp.concatenate([prob_sum, first_load] + [zero] * 6, axis=0)

    @pl.loop(1, 16)
    def _(i):
        stat_xy(i).start()

    @pl.loop(0, NC)
    def _(c):
        tok_twin(0, c).wait_recv()

    meta_wait(0)
    pack(0)
    scatter(0)

    @pl.loop(0, NC)
    def _(c):
        for u in range(2):
            tok_z(u, 0, c).wait_recv()
            tok_z(u, 1, c).start()
            tok_twin(1 + u, c).start()

    for idx in (1, 2):
        @pl.loop(0, NC)
        def _(c):
            tok_twin(idx, c).wait_recv()

        meta_wait(idx)
        pack(idx)
        scatter(idx)

    remote(STA.at[0:120], STA.at[0:120], sts.at[0], str_.at[0], expert_2=kt).wait_recv()
    STB[rows(z * 8, 8), :] = sum(STA[8 * i : 8 * i + 8, :] for i in range(16))

    @pl.loop(1, 8)
    def _(i):
        stat_z(i).start()

    loads[2].wait()
    loads[3].wait()
    tiles(0).wait_recv()
    ffn(0, 1)
    scatter_back(0)
    for idx in (3, 4):
        meta_wait(idx)
    for u in range(2):
        one_hot(PMK, u * 192, 128, 3 + u, (zn[u] * 2 + k) * 128)
        one_hot(PMK, u * 192 + 128, 64, 3 + u, (zn2[u] * 2 + k) * 128 + u * 64)

    @pl.loop(0, NC)
    def _(c):
        for u in range(2):
            tok_z(u, 1, c).wait_recv()
            tok_twin(3 + u, c).start()
        for u in range(2):
            tok_twin(3 + u, c).wait_recv()
            PK[u * 192 : u * 192 + 192, cols(c)] = jnp.dot(
                PMK[u * 192 : u * 192 + 192, :], T2[(3 + u) * 512 : (4 + u) * 512, cols(c)],
                preferred_element_type=F32,
            ).astype(BF)
            slots_z(u, True, c).start()
            slots_z(u, False, c).start()

    for idx in (3, 4):
        pack(idx)
        scatter(idx)
    for idx in (1, 2):
        tiles(idx).wait_recv()
    ffn(1, 2)
    for idx in (1, 2):
        scatter_back(idx)
    for idx in (3, 4):
        tiles(idx).wait_recv()
    ffn(3, 2)
    for idx in (3, 4):
        scatter_back(idx)

    remote(STB.at[0:56], STB.at[0:56], sts.at[1], str_.at[1], expert_2=kt).wait_recv()
    STC[rows(k * 8, 8), :] = sum(STB[8 * i : 8 * i + 8, :] for i in range(8))
    stat_twin().start()

    for n in range(3):
        tiles_back(n).wait_recv()
        back_twin1(n).start()

    for d in range(2):
        sign = 1.0 if d == 0 else -1.0
        s1, s2, g1, g2, e1, e2 = meta_cols(3 + d)
        e1, e2 = sign * e1, sign * e2
        w1, w2 = weights(e1, e2, 2.0, g1, g2)
        j = iota((1, 640), 1)
        p = jnp.where(j >= 320, 1, 0)
        r = j - 320 * p
        code = p * 128 + jnp.where(
            r < 128, z * 256 + r,
            jnp.where(r < 256, zn[d] * 256 + r - 128, zn2[d] * 256 + d * 64 + r - 256),
        )
        C2[d * 256 : d * 256 + 256, :] = placed(code.astype(F32), s1, s2, w1, w2)
        s1, s2, g1, g2, e1, e2 = meta_cols(1 + d)
        e1, e2 = sign * e1, sign * e2
        w1, w2 = weights(e1, e2, 1.0, g1, g2)
        near = (iota((1, 256), 1) + z * 256).astype(F32)
        C1[d * 256 : d * 256 + 256, 0:256] = placed(near, s1, s2, w1, w2)
        C1[d * 256 : d * 256 + 256, 256:512] = diagonal(passed(e1, e2, 2.0, w1, w2))
    s1, s2, g1, g2, e1, e2 = meta_cols(0)
    near = (iota((1, 256), 1) + z * 256).astype(F32)
    C0[:, 0:256] = placed(near, s1, s2, g1, g2)
    C0[:, 256:512] = diagonal(passed(e1, e2, 1.0, g1, g2))
    C0[:, 512:768] = diagonal(passed(-e1, -e2, 1.0, g1, g2))

    for u in range(2):
        @pl.loop(0, NC)
        def _(c):
            slots_z(u, True, c).wait_recv()

    scatter(7)
    for u in range(2):
        @pl.loop(0, NC)
        def _(c):
            slots_z(u, False, c).wait_recv()

        scatter(5 + u)
    for idx in (5, 6):
        tiles(idx).wait_recv()
    ffn(5, 2)
    for idx in (5, 6):
        scatter_back(idx)
    tiles(7).wait_recv()
    ffn(7, 1)
    scatter_back(7)

    for d in range(2):
        tiles_back(5 + d).wait_recv()

        @pl.loop(0, NC)
        def _(c):
            back_z(d, False, c).start()

    tiles_back(7).wait_recv()

    @pl.loop(0, NC)
    def _(c):
        back_z(0, True, c).start()
        back_z(1, True, c).start()

    for d in range(2):
        tiles_back(3 + d).wait_recv()

    @pl.loop(0, NC)
    def _(c):
        for d in range(2):
            back_z(d, False, c).wait_recv()
            back_z(d, True, c).wait_recv()
            back_twin2(d, c).start()
        for d in range(2):
            back_twin2(d, c).wait_recv()
            V2[d * 256 : d * 256 + 256, cols(c)] = jnp.dot(
                C2[d * 256 : d * 256 + 256, :], RB[S2 + d * 640 : S2 + d * 640 + 640, cols(c)],
                preferred_element_type=F32,
            ).astype(BF)
            mixed2(d, c).start()

    for n in range(3):
        back_twin1(n).wait_recv()

    @pl.loop(0, NC)
    def _(c):
        for d in range(2):
            mixed2(d, c).wait_recv()
            V1[d * 256 : d * 256 + 256, cols(c)] = jnp.dot(
                C1[d * 256 : d * 256 + 256, :], RB[S1 + d * 512 : S1 + d * 512 + 512, cols(c)],
                preferred_element_type=F32,
            ).astype(BF)
            mixed1(d, c).start()

    stat_twin().wait_recv()
    total = STC[0:8, :] + STC[8:16, :]
    count = 65536.0
    share = (total[0:1, :] / count) * (total[1:2, :] / count)
    aux[...] = jnp.broadcast_to(256.0 * jnp.sum(share, axis=1, keepdims=True), (8, 128))

    @pl.loop(0, NC)
    def _(c):
        for d in range(2):
            mixed1(d, c).wait_recv()
        out[:, cols(c)] = jnp.dot(
            C0[...], RB[S0 : S0 + 768, cols(c)], preferred_element_type=F32
        ).astype(BF)

    @pl.loop(0, NC)
    def _(c):
        for u in range(2):
            tok_z(u, 0, c).wait_send()
            tok_z(u, 1, c).wait_send()
            slots_z(u, False, c).wait_send()
            slots_z(u, True, c).wait_send()
            back_z(u, False, c).wait_send()
            back_z(u, True, c).wait_send()
            back_twin2(u, c).wait_send()
            mixed2(u, c).wait_send()
            mixed1(u, c).wait_send()
        for idx in range(5):
            tok_twin(idx, c).wait_send()

    for n in range(9):
        meta_to(n).wait_send()
    for n in range(3):
        back_twin1(n).wait_send()
    for idx in range(8):
        tiles(idx).wait_send()
        tiles_back(idx).wait_send()
    remote(STA.at[0:120], STA.at[0:120], sts.at[0], str_.at[0], expert_2=kt).wait_send()
    remote(STB.at[0:56], STB.at[0:56], sts.at[1], str_.at[1], expert_2=kt).wait_send()
    stat_twin().wait_send()


def shards(tokens, routes, priority, router, w_in, w_out):
    anywhere = pl.BlockSpec(memory_space=pl.ANY)
    vmem = pl.BlockSpec(memory_space=pltpu.VMEM)
    dma = pltpu.SemaphoreType.DMA
    mixed, aux = pl.pallas_call(
        kernel,
        out_shape=(
            jax.ShapeDtypeStruct((256, D), BF),
            jax.ShapeDtypeStruct((8, 128), F32),
        ),
        in_specs=[anywhere, vmem, vmem, anywhere, anywhere, anywhere],
        out_specs=(vmem, vmem),
        scratch_shapes=[
            pltpu.VMEM((10 * 256, D), BF),
            pltpu.VMEM((8 * 128, D), BF),
            pltpu.VMEM((2 * 192, D), BF),
            pltpu.VMEM((8 * 128, D), BF),
            pltpu.VMEM((8 * 128, D), BF),
            pltpu.VMEM((RB_ROWS, D), BF),
            pltpu.VMEM((2 * 256, D), BF),
            pltpu.VMEM((2 * 256, D), BF),
            pltpu.VMEM((D, FF), BF),
            pltpu.VMEM((D, FF), BF),
            pltpu.VMEM((D, 256), BF),
            pltpu.VMEM((256, FF), BF),
            pltpu.VMEM((128, 512), BF),
            pltpu.VMEM((2 * 192, 512), BF),
            pltpu.VMEM((2 * 256, 640), BF),
            pltpu.VMEM((2 * 256, 512), BF),
            pltpu.VMEM((256, 768), BF),
            pltpu.VMEM((10 * 8, 256), F32),
            pltpu.VMEM((16 * 8, 256), F32),
            pltpu.VMEM((8 * 8, 256), F32),
            pltpu.VMEM((2 * 8, 256), F32),
            dma((4,)),
            dma((2, 2, NC)), dma((2, 2, NC)),
            dma((5, NC)), dma((5, NC)),
            dma((2, 2, NC)), dma((2, 2, NC)),
            dma((9,)), dma((10,)),
            dma((8,)), dma((8,)),
            dma((8,)), dma((8,)),
            dma((3,)), dma((3,)),
            dma((2, 2, NC)), dma((2, 2, NC)),
            dma((2, NC)), dma((2, NC)),
            dma((3,)), dma((3,)),
            dma((2, NC)), dma((2, NC)),
            dma((2, NC)), dma((2, NC)),
        ],
        compiler_params=pltpu.CompilerParams(
            collective_id=0, has_side_effects=True, vmem_limit_bytes=64_000_000
        ),
    )(tokens, routes.T, priority, router, w_in[0], w_out[0])
    return mixed, aux[0, 0]


def solution(mesh):
    torus = Mesh(mesh.devices.reshape(4, 8, 2, mesh.shape["dp"]), EXPERT_DP)
    in_specs = (
        P(EXPERT_DP, None),
        P(EXPERT_DP, None),
        P(EXPERT_DP, None),
        P(),
        P(EXPERT_DP, None, None),
        P(EXPERT_DP, None, None),
    )
    return jax.shard_map(
        shards, mesh=torus, in_specs=in_specs, out_specs=(P(EXPERT_DP, None), P()), check_vma=False
    )
```

time: 296 us -> 217 us (0.73)
  blocking collectives: 228 us -> 0 us
  Pallas kernels: 0 us -> 213 us
  matrix products: 26 us -> 0 us
  local copies, waits for them, and re-layouts: 29 us -> 3.49 us
  starting transfers between devices: 7.97 us -> 0 us
    pallas_call x0 -> x1, Pallas kernels: none -> 213 us  [shards(): pl.pallas_call(kernel, out_shape=(jax.ShapeDtypeStruct((256, D), BF), jax...]
    all_to_all x1 -> x0, blocking collectives: 115 us -> none  [joined_exchange(): lax.all_to_all(pieces, axis, split_axis=0, concat_axis=0, tiled=True)]
    psum x4 -> x0, blocking collectives: 113 us -> none  [by_axis(): shard = lax.psum(shard, axis)]
    another operation x4 -> x0, local copies, waits for them, and re-layouts: 28.2 us -> none  [the longest x2 14.4 us: joined_exchange(): pieces = pieces.reshape(-1, *inside)]
    dot_general x7 -> x0, matrix products: 26 us -> none  [the longest x1 8.08 us: shards(): jnp.dot(expert_rows, w_in[0], preferred_element_type=jnp.float32)]
    all_to_all x1 -> x0, starting transfers between devices: 7.97 us -> none  [joined_exchange(): lax.all_to_all(pieces, axis, split_axis=0, concat_axis=0, tiled=True)]
  transfers between devices with their start and end apart: 1 -> 0, of which waited for: 0 -> 0; matrix products, arithmetic and copies ran while one was open for 0% -> 0% of each run, Pallas kernels for 0% -> 0%
where the time goes in v1:
time: 217 us
  Pallas kernels  213 us (98%)
  local copies, waits for them, and re-layouts  3.49 us (2%)
    pallas_call x1, Pallas kernels, shards(): pl.pallas_call(kernel, out_shape=(jax.ShapeDtypeStruct((256, D), BF), jax...  213 us

profile of v1, /device:TPU:1, one launch (start us, length us, event | category | flops | bytes accessed | tf_op | source)
XLA Modules:
  0.0 216.7 jit_solution(481830233341537681)
XLA Ops:
  0.6 212.6 %shard_map.77 = (bf16[256,2048]{1,0:T(8,128)(2,1)}, f32[8,128]{1,0:T(8,128)}) custom-call(bf16[256,2048]{1,0:T(8,128)(2,1)} %t_hbm.1, s32[2,256]{1,0:T(2,128)} %bitcast.6, s32[1,256]{1,0:T(1,128)} %ranks.1, bf16[2048,256]{1,0:T(8,128)(2,1)} %router_hbm.1, bf16[2048,1024]{1,0:T(8,128)(2,1)} %bitcast.4, bf16[2048,1024]{1,0:T(8,128)(2,1)} %bitcast.5), custom_call_target="tpu_custom_call" | custom-call | tf_op jit(solution)/shard_map/pallas_call | solution.py:571
  213.2 1.2 slice.3
  214.4 2.3 %copy.9 = bf16[256,2048]{1,0:T(8,128)(2,1)} copy(bf16[256,2048]{1,0:T(8,128)(2,1)} %get-tuple-element.8) | data formatting | bytes 2097152

commit v2 on v1

--- a/solution.py
+++ b/solution.py
@@ -67,7 +67,8 @@
 
     def xy(i):
         d = lax.rem(me + i, 16)
-        return d, {"expert_0": d // 4, "dp": lax.rem(d, 4)}
+        dx = lax.div(d, 4)
+        return d, {"expert_0": dx, "dp": d - 4 * dx}
 
     loads = [
         pltpu.make_async_copy(t_hbm, T2.at[rows(k * 256, 256)], ld.at[0]),
@@ -139,10 +140,11 @@
             r = rows((idx * 2 + kk) * 8, 8)
             remote(M.at[r], M.at[r], ms.at[0], mr.at[idx * 2 + kk], expert_2=kt).wait_recv()
 
-    def tile_out(idx, i):
+    def tile_out(idx, i, c):
         d, where = xy(i)
         return remote(
-            SRC.at[rows(idx * 128 + d * 8, 8)], X.at[rows(idx * 128 + me * 8, 8)],
+            SRC.at[rows(idx * 128 + d * 8, 8), cols(c)],
+            X.at[rows(idx * 128 + me * 8, 8), cols(c)],
             xs.at[idx], xr.at[idx], **where,
         )
 
@@ -150,13 +152,15 @@
         r = rows(idx * 128, 120)
         return remote(SRC.at[r], X.at[r], xs.at[idx], xr.at[idx], expert_2=kt)
 
-    def scatter(idx):
+    def scatter(idxs, c):
         @pl.loop(1, 16)
         def _(i):
-            tile_out(idx, i).start()
-
-        own = rows(idx * 128 + me * 8, 8)
-        X[own, :] = SRC[own, :]
+            for idx in idxs:
+                tile_out(idx, i, c).start()
+
+        for idx in idxs:
+            own = rows(idx * 128 + me * 8, 8)
+            X[own, cols(c)] = SRC[own, cols(c)]
 
     def home_row(idx):
         if idx == 0:
@@ -167,25 +171,30 @@
             return S2 + (idx - 3) * 640 + k * 320
         return RX + (idx - 5) * 128
 
-    def tile_back(idx, i):
+    def tile_back(idx, i, c):
         d, where = xy(i)
         return remote(
-            Y.at[rows(idx * 128 + d * 8, 8)], RB.at[rows(home_row(idx) + me * 8, 8)],
-            ys.at[idx], yr.at[idx], **where,
-        )
-
-    def tiles_back(idx):
-        return remote(
-            Y.at[rows(idx * 128, 120)], RB.at[rows(home_row(idx), 120)], ys.at[idx], yr.at[idx],
-            expert_2=kt,
-        )
-
-    def scatter_back(idx):
+            Y.at[rows(idx * 128 + d * 8, 8), cols(c)],
+            RB.at[rows(home_row(idx) + me * 8, 8), cols(c)],
+            ys.at[idx, c], yr.at[idx, c], **where,
+        )
+
+    def tiles_back(idx, c):
+        return remote(
+            Y.at[rows(idx * 128, 120), cols(c)], RB.at[rows(home_row(idx), 120), cols(c)],
+            ys.at[idx, c], yr.at[idx, c], expert_2=kt,
+        )
+
+    def scatter_back(idxs, c):
         @pl.loop(1, 16)
         def _(i):
-            tile_back(idx, i).start()
-
-        RB[rows(home_row(idx) + me * 8, 8), :] = Y[rows(idx * 128 + me * 8, 8), :]
+            for idx in idxs:
+                tile_back(idx, i, c).start()
+
+        for idx in idxs:
+            RB[rows(home_row(idx) + me * 8, 8), cols(c)] = Y[
+                rows(idx * 128 + me * 8, 8), cols(c)
+            ]
 
     def back_z(d, far, c):
         if far:
@@ -204,9 +213,11 @@
         r = rows(S2 + d * 640 + k * 320, 320)
         return remote(RB.at[r, cols(c)], RB.at[r, cols(c)], es.at[d, c], er.at[d, c], expert_2=kt)
 
-    def back_twin1(n):
+    def back_twin1(n, c):
         r = rows(home_row(n), 128)
-        return remote(RB.at[r], RB.at[r], t1s.at[n], t1r.at[n], expert_2=kt)
+        return remote(
+            RB.at[r, cols(c)], RB.at[r, cols(c)], t1s.at[n, c], t1r.at[n, c], expert_2=kt
+        )
 
     def mixed2(d, c):
         return remote(
@@ -242,30 +253,32 @@
             hit = (code == M[r : r + 1, :]) | (code == M[r + 1 : r + 2, :])
             dst[row0 : row0 + count, g * 256 : (g + 1) * 256] = jnp.where(hit, 1.0, 0.0).astype(BF)
 
-    def pack(idx):
-        one_hot(PM, 0, 128, idx, (z * 2 + k) * 128)
+    def pack(idx, slot, c):
+        SRC[idx * 128 : idx * 128 + 128, cols(c)] = jnp.dot(
+            PM[slot * 128 : slot * 128 + 128, :], T2[idx * 512 : idx * 512 + 512, cols(c)],
+            preferred_element_type=F32,
+        ).astype(BF)
+
+    def ffn_in(idx, count):
+        r = pl.ds(idx * 128, count * 128)
+
+        @pl.loop(0, FF // 512)
+        def _(n):
+            part = jnp.dot(X[r, :], W1[:, cols(n, 512)], preferred_element_type=F32)
+            H[0 : count * 128, cols(n, 512)] = jnp.maximum(part, 0.0).astype(BF)
+
+    def ffn_out(idx, count, c):
+        Y[idx * 128 : (idx + count) * 128, cols(c)] = lax.dot_general(
+            H[0 : count * 128, :], W2[cols(c), :],
+            (((1,), (1,)), ((), ())), preferred_element_type=F32,
+        ).astype(BF)
+
+    def ffn(idx, count):
+        ffn_in(idx, count)
 
         @pl.loop(0, NC)
         def _(c):
-            SRC[idx * 128 : idx * 128 + 128, cols(c)] = jnp.dot(
-                PM[...], T2[idx * 512 : idx * 512 + 512, cols(c)], preferred_element_type=F32
-            ).astype(BF)
-
-    def ffn(idx, count):
-        r = pl.ds(idx * 128, count * 128)
-        h = pl.ds(0, count * 128)
-
-        @pl.loop(0, FF // 256)
-        def _(n):
-            part = jnp.dot(X[r, :], W1[:, cols(n, 256)], preferred_element_type=F32)
-            H[h, cols(n, 256)] = jnp.maximum(part, 0.0).astype(BF)
-
-        @pl.loop(0, D // 256)
-        def _(n):
-            Y[r, cols(n, 256)] = lax.dot_general(
-                H[h, :], W2[pl.ds(pl.multiple_of(n * 256, 256), 256), :],
-                (((1,), (1,)), ((), ())), preferred_element_type=F32,
-            ).astype(BF)
+            ffn_out(idx, count, c)
 
     def meta_cols(idx):
         block = M[rows((idx * 2 + k) * 8, 8), :]
@@ -355,13 +368,19 @@
     def _(i):
         stat_xy(i).start()
 
+    plane = (z * 2 + k) * 128
+    meta_wait(0)
+    one_hot(PM, 0, 128, 0, plane)
+
     @pl.loop(0, NC)
     def _(c):
         tok_twin(0, c).wait_recv()
-
-    meta_wait(0)
-    pack(0)
-    scatter(0)
+        pack(0, 0, c)
+        scatter((0,), c)
+
+    for idx in (1, 2):
+        meta_wait(idx)
+        one_hot(PM, (idx - 1) * 128, 128, idx, plane)
 
     @pl.loop(0, NC)
     def _(c):
@@ -369,15 +388,10 @@
             tok_z(u, 0, c).wait_recv()
             tok_z(u, 1, c).start()
             tok_twin(1 + u, c).start()
-
-    for idx in (1, 2):
-        @pl.loop(0, NC)
-        def _(c):
-            tok_twin(idx, c).wait_recv()
-
-        meta_wait(idx)
-        pack(idx)
-        scatter(idx)
+        for u in range(2):
+            tok_twin(1 + u, c).wait_recv()
+            pack(1 + u, u, c)
+        scatter((1, 2), c)
 
     remote(STA.at[0:120], STA.at[0:120], sts.at[0], str_.at[0], expert_2=kt).wait_recv()
     STB[rows(z * 8, 8), :] = sum(STA[8 * i : 8 * i + 8, :] for i in range(16))
@@ -388,14 +402,19 @@
 
     loads[2].wait()
     loads[3].wait()
-    tiles(0).wait_recv()
-    ffn(0, 1)
-    scatter_back(0)
     for idx in (3, 4):
         meta_wait(idx)
+        one_hot(PM, (idx - 3) * 128, 128, idx, plane)
     for u in range(2):
         one_hot(PMK, u * 192, 128, 3 + u, (zn[u] * 2 + k) * 128)
         one_hot(PMK, u * 192 + 128, 64, 3 + u, (zn2[u] * 2 + k) * 128 + u * 64)
+    tiles(0).wait_recv()
+    ffn_in(0, 1)
+
+    @pl.loop(0, NC)
+    def _(c):
+        ffn_out(0, 1, c)
+        scatter_back((0,), c)
 
     @pl.loop(0, NC)
     def _(c):
@@ -410,28 +429,37 @@
             ).astype(BF)
             slots_z(u, True, c).start()
             slots_z(u, False, c).start()
-
-    for idx in (3, 4):
-        pack(idx)
-        scatter(idx)
+        for u in range(2):
+            pack(3 + u, u, c)
+        scatter((3, 4), c)
+
     for idx in (1, 2):
         tiles(idx).wait_recv()
     ffn(1, 2)
-    for idx in (1, 2):
-        scatter_back(idx)
+
+    def far_slots(c):
+        for u in range(2):
+            slots_z(u, True, c).wait_recv()
+            slots_z(u, False, c).wait_recv()
+        scatter((5, 6, 7), c)
+
+    @pl.loop(0, NC - 1)
+    def _(c):
+        far_slots(c)
+
     for idx in (3, 4):
         tiles(idx).wait_recv()
     ffn(3, 2)
-    for idx in (3, 4):
-        scatter_back(idx)
+    far_slots(NC - 1)
 
     remote(STB.at[0:56], STB.at[0:56], sts.at[1], str_.at[1], expert_2=kt).wait_recv()
     STC[rows(k * 8, 8), :] = sum(STB[8 * i : 8 * i + 8, :] for i in range(8))
     stat_twin().start()
 
-    for n in range(3):
-        tiles_back(n).wait_recv()
-        back_twin1(n).start()
+    @pl.loop(0, NC)
+    def _(c):
+        tiles_back(0, c).wait_recv()
+        back_twin1(0, c).start()
 
     for d in range(2):
         sign = 1.0 if d == 0 else -1.0
@@ -458,47 +486,32 @@
     C0[:, 256:512] = diagonal(passed(e1, e2, 1.0, g1, g2))
     C0[:, 512:768] = diagonal(passed(-e1, -e2, 1.0, g1, g2))
 
-    for u in range(2):
-        @pl.loop(0, NC)
-        def _(c):
-            slots_z(u, True, c).wait_recv()
-
-    scatter(7)
-    for u in range(2):
-        @pl.loop(0, NC)
-        def _(c):
-            slots_z(u, False, c).wait_recv()
-
-        scatter(5 + u)
-    for idx in (5, 6):
+    for idx in (5, 6, 7):
         tiles(idx).wait_recv()
-    ffn(5, 2)
-    for idx in (5, 6):
-        scatter_back(idx)
-    tiles(7).wait_recv()
-    ffn(7, 1)
-    scatter_back(7)
-
-    for d in range(2):
-        tiles_back(5 + d).wait_recv()
-
-        @pl.loop(0, NC)
-        def _(c):
+    ffn_in(5, 3)
+
+    @pl.loop(0, NC)
+    def _(c):
+        ffn_out(5, 3, c)
+        scatter_back((5, 6, 7), c)
+
+    @pl.loop(0, NC)
+    def _(c):
+        for idx in (5, 6, 7):
+            tiles_back(idx, c).wait_recv()
+        for d in range(2):
+            back_z(d, True, c).start()
             back_z(d, False, c).start()
-
-    tiles_back(7).wait_recv()
-
-    @pl.loop(0, NC)
-    def _(c):
-        back_z(0, True, c).start()
-        back_z(1, True, c).start()
-
-    for d in range(2):
-        tiles_back(3 + d).wait_recv()
+        scatter_back((3, 4), c)
+
+    @pl.loop(0, NC)
+    def _(c):
+        scatter_back((1, 2), c)
 
     @pl.loop(0, NC)
     def _(c):
         for d in range(2):
+            tiles_back(3 + d, c).wait_recv()
             back_z(d, False, c).wait_recv()
             back_z(d, True, c).wait_recv()
             back_twin2(d, c).start()
@@ -510,8 +523,16 @@
             ).astype(BF)
             mixed2(d, c).start()
 
-    for n in range(3):
-        back_twin1(n).wait_recv()
+    @pl.loop(0, NC)
+    def _(c):
+        for n in (1, 2):
+            tiles_back(n, c).wait_recv()
+            back_twin1(n, c).start()
+
+    @pl.loop(0, NC)
+    def _(c):
+        for n in range(3):
+            back_twin1(n, c).wait_recv()
 
     @pl.loop(0, NC)
     def _(c):
@@ -527,7 +548,7 @@
     total = STC[0:8, :] + STC[8:16, :]
     count = 65536.0
     share = (total[0:1, :] / count) * (total[1:2, :] / count)
-    aux[...] = jnp.broadcast_to(256.0 * jnp.sum(share, axis=1, keepdims=True), (8, 128))
+    aux[0, 0] = 256.0 * jnp.sum(share)
 
     @pl.loop(0, NC)
     def _(c):
@@ -551,14 +572,15 @@
             mixed1(u, c).wait_send()
         for idx in range(5):
             tok_twin(idx, c).wait_send()
+        for n in range(3):
+            back_twin1(n, c).wait_send()
+        for idx in range(8):
+            tiles_back(idx, c).wait_send()
 
     for n in range(9):
         meta_to(n).wait_send()
-    for n in range(3):
-        back_twin1(n).wait_send()
     for idx in range(8):
         tiles(idx).wait_send()
-        tiles_back(idx).wait_send()
     remote(STA.at[0:120], STA.at[0:120], sts.at[0], str_.at[0], expert_2=kt).wait_send()
     remote(STB.at[0:56], STB.at[0:56], sts.at[1], str_.at[1], expert_2=kt).wait_send()
     stat_twin().wait_send()
@@ -571,11 +593,11 @@
     mixed, aux = pl.pallas_call(
         kernel,
         out_shape=(
-            jax.ShapeDtypeStruct((256, D), BF),
-            jax.ShapeDtypeStruct((8, 128), F32),
+            pltpu.VMEM((256, D), BF),
+            jax.ShapeDtypeStruct((1, 1), F32),
         ),
         in_specs=[anywhere, vmem, vmem, anywhere, anywhere, anywhere],
-        out_specs=(vmem, vmem),
+        out_specs=(vmem, pl.BlockSpec(memory_space=pltpu.SMEM)),
         scratch_shapes=[
             pltpu.VMEM((10 * 256, D), BF),
             pltpu.VMEM((8 * 128, D), BF),
@@ -588,8 +610,8 @@
             pltpu.VMEM((D, FF), BF),
             pltpu.VMEM((D, FF), BF),
             pltpu.VMEM((D, 256), BF),
-            pltpu.VMEM((256, FF), BF),
-            pltpu.VMEM((128, 512), BF),
+            pltpu.VMEM((3 * 128, FF), BF),
+            pltpu.VMEM((2 * 128, 512), BF),
             pltpu.VMEM((2 * 192, 512), BF),
             pltpu.VMEM((2 * 256, 640), BF),
             pltpu.VMEM((2 * 256, 512), BF),
@@ -604,11 +626,11 @@
             dma((2, 2, NC)), dma((2, 2, NC)),
             dma((9,)), dma((10,)),
             dma((8,)), dma((8,)),
-            dma((8,)), dma((8,)),
+            dma((8, NC)), dma((8, NC)),
             dma((3,)), dma((3,)),
             dma((2, 2, NC)), dma((2, 2, NC)),
             dma((2, NC)), dma((2, NC)),
-            dma((3,)), dma((3,)),
+            dma((3, NC)), dma((3, NC)),
             dma((2, NC)), dma((2, NC)),
             dma((2, NC)), dma((2, NC)),
         ],

time: 217 us -> 181 us (0.83); the launches traced: 217 us -> 178 us
  Pallas kernels: 213 us -> 175 us
  local copies, waits for them, and re-layouts: 3.49 us -> 0.97 us
    pallas_call x1, Pallas kernels: 213 us -> 175 us  [shards(): pl.pallas_call(kernel, out_shape=(pltpu.VMEM((256, D), BF), jax.ShapeDtyp...]
where the time goes in v2:
time: 181 us; the launch traced here: 178 us
  Pallas kernels  175 us (97%)
  between operations  2.33 us (1%)
    pallas_call x1, Pallas kernels, shards(): pl.pallas_call(kernel, out_shape=(pltpu.VMEM((256, D), BF), jax.ShapeDtyp...  175 us

profile of v2, /device:TPU:1, one launch (start us, length us, event | category | flops | bytes accessed | tf_op | source)
XLA Modules:
  0.0 178.3 jit_solution(6142208917508422349)
XLA Ops:
  0.6 175.0 %shard_map.77 = (bf16[256,2048]{1,0:T(8,128)(2,1)S(1)}, f32[1,1]{1,0:T(1,128)}) custom-call(bf16[256,2048]{1,0:T(8,128)(2,1)} %t_hbm.1, s32[2,256]{1,0:T(2,128)} %bitcast.6, s32[1,256]{1,0:T(1,128)} %ranks.1, bf16[2048,256]{1,0:T(8,128)(2,1)} %router_hbm.1, bf16[2048,1024]{1,0:T(8,128)(2,1)} %bitcast.4, bf16[2048,1024]{1,0:T(8,128)(2,1)} %bitcast.5), custom_call_target="tpu_custom_call" | custom-call | tf_op jit(solution)/shard_map/pallas_call | solution.py:593
  175.6 1.0 copy.10
